TPU v7x, 32 devices: a whole 2x2x4 slice. The times are simulated.
32 devices in a mesh: genes: 16 (over z, y, core), cols: 2 (over x).
Axes of the slice: x: 2, y: 2, z: 4, core: 2. Of those that a mesh axis runs over, the one named last changes fastest.
Arguments:
- expression: float32 [384, 40960], P(None, ('genes', 'cols')), may hold values from -200 to 200
- resample: int32 [384], replicated, may hold values from 0 to 383
- labels: int32 [40960, 300], P(('genes', 'cols')), may hold values from 0 to 1, as said below
- ref_kim: float32 [40960], P(('genes', 'cols')), may hold values from 0 to 1
Outputs:
- connectivity: float32 [40960, 300], P(('genes', 'cols'))
- preservation: float32 [2, 300], replicated
Inputs may be any that keep to these rules, and one draw needn't show every extreme that they name: `labels`: each row holds exactly one 1; every module has 32 or more genes.
All inputs are finite; a program needn't handle non-finite values.
Results may differ from a plain program's by a relative error of at most 0.0031.
Values may be sent and summed in bfloat16 or wider, within the bound.
A program may use at most 128 MiB of HBM per device.

v0:
```python
import math
import jax
import jax.numpy as jnp
from jax import lax
from jax.sharding import PartitionSpec as P

G = 40960


def standardize(expression, resample):
    boot = jnp.take(expression, resample, axis=0)
    centered = boot - jnp.mean(boot, axis=0, keepdims=True)
    total = jnp.sum(centered * centered, axis=0, keepdims=True)
    return (centered * lax.rsqrt(total + 1e-06)).astype(jnp.bfloat16)


def local_sums(connectivity, labels, ref_kim):
    member = labels.astype(jnp.float32)
    kim = jnp.sum(connectivity * member, axis=1)
    rowsum = jnp.sum(connectivity, axis=1)
    stacked = jnp.stack(
        [kim, kim * kim, ref_kim, ref_kim * ref_kim, kim * ref_kim, rowsum, jnp.ones_like(kim)],
        axis=1,
    )
    return jnp.dot(
        member.T, stacked, precision=lax.Precision.HIGHEST, preferred_element_type=jnp.float32
    )


def preserve(sums, total_genes):
    counts = sums[:, 6]
    mean_x = sums[:, 0] / (counts * counts)
    var_x = jnp.maximum(sums[:, 1] / (counts * counts * counts) - mean_x * mean_x, 0.0001)
    mean_y = sums[:, 2] / counts
    var_y = jnp.maximum(sums[:, 3] / counts - mean_y * mean_y, 0.01)
    cross = sums[:, 4] / (counts * counts) - mean_x * mean_y
    between = (sums[:, 5] - sums[:, 0]) / (counts * (total_genes - counts))
    density = (mean_x - between) * jnp.sqrt(counts / var_x)
    linked = cross * jnp.sqrt(counts / (var_x * var_y))
    return jnp.stack([density, linked], axis=0)


def tile_term(row_block, column_block, column_ids, module_count):
    scores = lax.dot_general(
        row_block, column_block, (((0,), (0,)), ((), ())), preferred_element_type=jnp.float32
    )
    squares = scores * scores
    adjacency = (squares * squares * squares).astype(jnp.bfloat16)
    member_block = (
        column_ids[:, None] == jnp.arange(module_count, dtype=jnp.int32)[None, :]
    ).astype(jnp.bfloat16)
    return jnp.dot(adjacency, member_block, preferred_element_type=jnp.float32)


def add_tiles(carried, row_block, piece, every_ids, shard_width, module_count):
    span_width = piece.shape[1]
    column_step = shard_width * math.gcd(span_width // shard_width, 8)
    steps_total = span_width // column_step

    def one_step(step_index, accumulated):
        columns = lax.dynamic_slice_in_dim(piece, step_index * column_step, column_step, 1)
        column_ids = lax.dynamic_slice_in_dim(every_ids, step_index * column_step, column_step, 0)
        return accumulated + tile_term(row_block, columns, column_ids, module_count)

    return lax.fori_loop(0, steps_total, one_step, carried)


def local(expression, resample, labels, ref_kim):
    scaled = standardize(expression, resample)
    module_count = labels.shape[1]
    shard_width = scaled.shape[1]
    module_ids = jnp.sum(labels * jnp.arange(module_count, dtype=jnp.int32)[None, :], axis=1)
    row_block = lax.all_gather(scaled, "cols", axis=1, tiled=True)
    panel_ids = lax.all_gather(module_ids, "genes", axis=0, tiled=True)
    initial = jnp.zeros((row_block.shape[1], module_count), jnp.float32)
    partial_value = add_tiles(
        initial,
        row_block,
        lax.all_gather(scaled, "genes", axis=1, tiled=True),
        panel_ids,
        shard_width,
        module_count,
    )
    connectivity = lax.psum_scatter(partial_value, "cols", scatter_dimension=0, tiled=True)
    sums = lax.psum(local_sums(connectivity, labels, ref_kim), ("genes", "cols"))
    return (connectivity, preserve(sums, G))


def solution(mesh):
    placed = (P(None, ("genes", "cols")), P(), P(("genes", "cols"), None), P(("genes", "cols")))
    return jax.shard_map(
        local,
        mesh=mesh,
        in_specs=placed,
        out_specs=(P(("genes", "cols"), None), P()),
        check_vma=False,
    )
```

profile of v0, /device:TPU:0, one launch (start us, length us, event | category | flops | bytes accessed | tf_op | source)
XLA Modules:
  0.0 391.7 jit_solution(1327400909456358095)
XLA Ops:
  7.2 0.8 compare_select_fusion
  8.0 0.7 compare_and_fusion
  8.8 2.7 gather_fusion
  11.5 1.9 select_reduce_fusion
  14.0 1.3 multiply_convert_fusion
  15.3 0.7 all-gather.4.cloned.1.call-update
  16.3 23.3 %all-gather = s32[16,1,1280]{2,1,0:T(1,128)S(1)} all-gather(s32[1,1,1280]{2,1,0:T(1,128)S(1)} %reshape.229), channel_id=1, replica_groups=mesh['genes'=16,'cols'=2] {'genes'}, dimensions={0}, use_global_device_ids=true | all-gather | bytes 87040 | tf_op jit(solution)/shard_map/all_gather | solution.py:74
  39.6 10.2 %all-gather.6.cloned.1.call-done = bf16[384,2560]{1,0:T(8,128)(2,1)} async-done(((bf16[384,1280]{1,0:T(8,128)(2,1)}), bf16[384,2560]{1,0:T(8,128)(2,1)}) %all-gather.6.cloned.1.call-update) | async-done | bytes 1966096 | tf_op jit(solution)/shard_map/all_gather | solution.py:73
  49.8 122.7 %all-gather.4.cloned.1.call-done = bf16[384,20480]{1,0:T(8,128)(2,1)} async-done(((bf16[384,1280]{1,0:T(8,128)(2,1)}), bf16[384,20480]{1,0:T(8,128)(2,1)}) %all-gather.4.cloned.1.call-update) | async-done | bytes 15728656 | tf_op jit(solution)/shard_map/all_gather | solution.py:79
  172.5 124.2 %while.14 = (s32[]{:T(128)}, f32[2560,300]{0,1:T(8,128)}, bf16[384,20480]{1,0:T(8,128)(2,1)}, bf16[384,2560]{1,0:T(8,128)(2,1)}, s32[20480]{0:T(1024)S(1)}, /*index=5*/s32[]{:T(128)}, s32[]{:T(128)}, s32[]{:T(128)}, s32[]{:T(128)}) while((s32[]{:T(128)}, f32[2560,300]{0,1:T(8,128)}, bf16[384,20480]{1,0:T(8,128)(2,1)}, ...), condition=%wide.region_4.5_spmd.clone, body=%wide.region_3.4_spmd.clone.sunk | while | flops 35970764800 | bytes 120955040 | solution.py:65
  172.5 37.4 %fusion.clone.9 = bf16[2560,10240]{0,1:T(8,128)(2,1)} fusion(bf16[384,2560]{1,0:T(8,128)(2,1)} %get-tuple-element.184, bf16[384,20480]{1,0:T(8,128)(2,1)} %get-tuple-element.183, s32[]{:T(128)S(6)} %select_n.27), kind=kOutput, calls=%fused_computation.2.clone.clone.clone.clone.clone.2.clone.1 | convolution fusion | flops 20237516800 | bytes 62259204 | tf_op jit(solution)/shard_map/while/body/eval_jaxpr/dot_general | solution.py:44
  209.9 24.2 %fusion.47 = f32[2560,300]{0,1:T(8,128)} fusion(s32[10240]{0:T(1024)S(1)} %dynamic_slice.28, f32[2560,300]{0,1:T(8,128)} %get-tuple-element.173, pred[]{:T(512)S(6)} %compare.3, bf16[2560,10240]{0,1:T(8,128)(2,1)} %fusion.clone.9), kind=kOutput, calls=%fused_computation.7.clone.3 | convolution fusion | flops 15733248000 | bytes 58613760 | tf_op jit(solution)/shard_map/while/body/eval_jaxpr/dot_general | solution.py:52
  234.1 37.4 %fusion.clone.9 = bf16[2560,10240]{0,1:T(8,128)(2,1)} fusion(bf16[384,2560]{1,0:T(8,128)(2,1)} %get-tuple-element.184, bf16[384,20480]{1,0:T(8,128)(2,1)} %get-tuple-element.183, s32[]{:T(128)S(6)} %select_n.27), kind=kOutput, calls=%fused_computation.2.clone.clone.clone.clone.clone.2.clone.1 | convolution fusion | flops 20237516800 | bytes 62259204 | tf_op jit(solution)/shard_map/while/body/eval_jaxpr/dot_general | solution.py:44
  271.6 25.1 %fusion.47 = f32[2560,300]{0,1:T(8,128)} fusion(s32[10240]{0:T(1024)S(1)} %dynamic_slice.28, f32[2560,300]{0,1:T(8,128)} %get-tuple-element.173, pred[]{:T(512)S(6)} %compare.3, bf16[2560,10240]{0,1:T(8,128)(2,1)} %fusion.clone.9), kind=kOutput, calls=%fused_computation.7.clone.3 | convolution fusion | flops 15733248000 | bytes 58613760 | tf_op jit(solution)/shard_map/while/body/eval_jaxpr/dot_general | solution.py:52
  296.7 0.7 copy-done.5
  297.4 40.6 %reduce-scatter.2.cloned.1.call-done = f32[1280,300]{0,1:T(8,128)} async-done(((f32[2560,300]{0,1:T(8,128)}), f32[1280,300]{0,1:T(8,128)}) %reduce-scatter.2.cloned.1.call-update) | async-done | bytes 1536016 | tf_op jit(solution)/shard_map/reduce_scatter | solution.py:84
  338.0 1.6 fusion.26
  339.7 0.6 stack.27
  340.3 0.6 stack.28
  340.9 0.6 stack_broadcast_in_dim.3
  341.5 1.4 stack.29
  342.9 2.1 fusion.12
  345.0 39.5 %psum.7 = f32[300,7]{0,1:T(8,128)S(1)} all-reduce(f32[300,7]{0,1:T(8,128)S(1)} %fusion.12), channel_id=1, replica_groups=mesh['genes'=16,'cols'=2] {'genes','cols'}, use_global_device_ids=true, to_apply=%region_8.9 | all-reduce | flops 2100 | bytes 16800 | tf_op jit(solution)/shard_map/psum | solution.py:85
  384.6 0.6 pad_maximum_fusion
  (32 shorter events, 1.0 us)
Async XLA Ops:
  7.2 1.6 copy-start
  7.2 42.6 %all-gather.6.cloned.1.call-start = ((), (), s32[]{:S(2)}) async-start(), calls=%async_computation.2 | async-start | bytes 2949120 | tf_op jit(solution)/shard_map/all_gather | solution.py:73
  11.5 2.1 copy-start.2
  14.0 2.1 copy-start.3
  15.3 157.2 %all-gather.4.cloned.1.call-start = ((), (), s32[]{:S(2)}) async-start(), calls=%async_computation.1 | async-start | bytes 16711680 | tf_op jit(solution)/shard_map/all_gather | solution.py:79
  16.0 322.0 %reduce-scatter.2.cloned.1.call-start = ((), (), s32[]{:S(2)}) async-start(), calls=%async_computation.3 | async-start | bytes 4669440 | tf_op jit(solution)/shard_map/reduce_scatter | solution.py:84
  296.7 0.7 copy-start.5
  296.7 41.4 %copy-start.4 = (s32[1280,300]{0,1:T(8,128)S(1)}, s32[1280,300]{0,1:T(8,128)}, u32[]{:S(2)}) copy-start(s32[1280,300]{0,1:T(8,128)} %param.8) | copy-start | bytes 4608004
  297.4 87.8 %copy-start.1 = (f32[384,1280]{1,0:T(8,128)S(1)}, f32[384,1280]{1,0:T(8,128)}, u32[]{:S(2)}) copy-start(f32[384,1280]{1,0:T(8,128)} %param.6) | copy-start | bytes 5898244
Sparse Core Ops, SparseCore 0:
  15.4 34.3 all-gather.5
  52.6 119.7 all-gather.3
  296.8 41.1 reduce-scatter.1
where the time goes:
time: 392 us
  waiting for transfers between devices  174 us (44%)
  matrix products  126 us (32%)
  blocking collectives  62.8 us (16%)
  between operations  13.9 us (4%)
  other arithmetic  7.47 us (2%)
  local copies, waits for them, and re-layouts  6.83 us (2%)
    all_gather x1, waiting for transfers between devices, local(): lax.all_gather(scaled, 'genes', axis=1, tiled=True)  123 us
    dot_general x2, matrix products, tile_term(): lax.dot_general(row_block, column_block, (((0,), (0,)), ((), ())), prefer...  74.9 us
    dot_general x2, matrix products, tile_term(): return jnp.dot(adjacency, member_block, preferred_element_type=jnp.float32)  49.3 us
    reduce_scatter x1, waiting for transfers between devices, local(): lax.psum_scatter(partial_value, 'cols', scatter_dimension=0, tiled=True)  40.6 us
    psum x1, blocking collectives, local(): lax.psum(local_sums(connectivity, labels, ref_kim), ('genes', 'cols'))  39.5 us
    all_gather x1, blocking collectives, local(): panel_ids = lax.all_gather(module_ids, 'genes', axis=0, tiled=True)  23.3 us
    all_gather x1, waiting for transfers between devices, local(): row_block = lax.all_gather(scaled, 'cols', axis=1, tiled=True)  10.2 us
  transfers between devices with their start and end apart: 3, of which 3 were waited for; matrix products, arithmetic and copies ran while one was open for 0% of the time, Pallas kernels for 0%

commit v1 on v0

--- a/solution.py
+++ b/solution.py
@@ -82,7 +82,9 @@
         module_count,
     )
     connectivity = lax.psum_scatter(partial_value, "cols", scatter_dimension=0, tiled=True)
-    sums = lax.psum(local_sums(connectivity, labels, ref_kim), ("genes", "cols"))
+    piece_in = local_sums(connectivity, labels, ref_kim)
+    reached = jax.lax.psum(piece_in, "cols")
+    sums = jax.lax.psum(reached, "genes")
     return (connectivity, preserve(sums, G))
 
 

time: 392 us -> 419 us (1.069)
  blocking collectives: 62.8 us -> 89.9 us
    psum x1 -> x2, blocking collectives: 39.5 us -> 66.5 us  [the longest x1 59.6 us: local(): sums = jax.lax.psum(reached, 'genes')]
where the time goes in v1:
time: 419 us
  waiting for transfers between devices  174 us (42%)
  matrix products  126 us (30%)
  blocking collectives  89.9 us (21%)
  between operations  13.9 us (3%)
  other arithmetic  7.47 us (2%)
  local copies, waits for them, and re-layouts  6.83 us (2%)
    all_gather x1, waiting for transfers between devices, local(): lax.all_gather(scaled, 'genes', axis=1, tiled=True)  123 us
    dot_general x2, matrix products, tile_term(): lax.dot_general(row_block, column_block, (((0,), (0,)), ((), ())), prefer...  74.9 us
    psum x1, blocking collectives, local(): sums = jax.lax.psum(reached, 'genes')  59.6 us
    dot_general x2, matrix products, tile_term(): return jnp.dot(adjacency, member_block, preferred_element_type=jnp.float32)  49.3 us
    reduce_scatter x1, waiting for transfers between devices, local(): lax.psum_scatter(partial_value, 'cols', scatter_dimension=0, tiled=True)  40.7 us
    all_gather x1, blocking collectives, local(): panel_ids = lax.all_gather(module_ids, 'genes', axis=0, tiled=True)  23.3 us
    all_gather x1, waiting for transfers between devices, local(): row_block = lax.all_gather(scaled, 'cols', axis=1, tiled=True)  10.2 us
  transfers between devices with their start and end apart: 3, of which 3 were waited for; matrix products, arithmetic and copies ran while one was open for 0% of the time, Pallas kernels for 0%

profile of v1, /device:TPU:0, one launch (start us, length us, event | category | flops | bytes accessed | tf_op | source)
XLA Modules:
  0.0 418.8 jit_solution(10145371595349270236)
XLA Ops:
  7.2 0.8 compare_select_fusion
  8.0 0.7 compare_and_fusion
  8.8 2.7 gather_fusion
  11.5 1.9 select_reduce_fusion
  14.0 1.3 multiply_convert_fusion
  15.3 0.7 all-gather.4.cloned.1.call-update
  16.3 23.3 %all-gather = s32[16,1,1280]{2,1,0:T(1,128)S(1)} all-gather(s32[1,1,1280]{2,1,0:T(1,128)S(1)} %reshape.229), channel_id=1, replica_groups=mesh['genes'=16,'cols'=2] {'genes'}, dimensions={0}, use_global_device_ids=true | all-gather | bytes 87040 | tf_op jit(solution)/shard_map/all_gather | solution.py:74
  39.6 10.2 %all-gather.6.cloned.1.call-done = bf16[384,2560]{1,0:T(8,128)(2,1)} async-done(((bf16[384,1280]{1,0:T(8,128)(2,1)}), bf16[384,2560]{1,0:T(8,128)(2,1)}) %all-gather.6.cloned.1.call-update) | async-done | bytes 1966096 | tf_op jit(solution)/shard_map/all_gather | solution.py:73
  49.8 122.7 %all-gather.4.cloned.1.call-done = bf16[384,20480]{1,0:T(8,128)(2,1)} async-done(((bf16[384,1280]{1,0:T(8,128)(2,1)}), bf16[384,20480]{1,0:T(8,128)(2,1)}) %all-gather.4.cloned.1.call-update) | async-done | bytes 15728656 | tf_op jit(solution)/shard_map/all_gather | solution.py:79
  172.5 124.2 %while.14 = (s32[]{:T(128)}, f32[2560,300]{0,1:T(8,128)}, bf16[384,20480]{1,0:T(8,128)(2,1)}, bf16[384,2560]{1,0:T(8,128)(2,1)}, s32[20480]{0:T(1024)S(1)}, /*index=5*/s32[]{:T(128)}, s32[]{:T(128)}, s32[]{:T(128)}, s32[]{:T(128)}) while((s32[]{:T(128)}, f32[2560,300]{0,1:T(8,128)}, bf16[384,20480]{1,0:T(8,128)(2,1)}, ...), condition=%wide.region_4.5_spmd.clone, body=%wide.region_3.4_spmd.clone.sunk | while | flops 35970764800 | bytes 120955040 | solution.py:65
  172.5 37.4 %fusion.clone.9 = bf16[2560,10240]{0,1:T(8,128)(2,1)} fusion(bf16[384,2560]{1,0:T(8,128)(2,1)} %get-tuple-element.184, bf16[384,20480]{1,0:T(8,128)(2,1)} %get-tuple-element.183, s32[]{:T(128)S(6)} %select_n.27), kind=kOutput, calls=%fused_computation.2.clone.clone.clone.clone.clone.2.clone.1 | convolution fusion | flops 20237516800 | bytes 62259204 | tf_op jit(solution)/shard_map/while/body/eval_jaxpr/dot_general | solution.py:44
  209.9 24.2 %fusion.47 = f32[2560,300]{0,1:T(8,128)} fusion(s32[10240]{0:T(1024)S(1)} %dynamic_slice.28, f32[2560,300]{0,1:T(8,128)} %get-tuple-element.173, pred[]{:T(512)S(6)} %compare.3, bf16[2560,10240]{0,1:T(8,128)(2,1)} %fusion.clone.9), kind=kOutput, calls=%fused_computation.7.clone.3 | convolution fusion | flops 15733248000 | bytes 58613760 | tf_op jit(solution)/shard_map/while/body/eval_jaxpr/dot_general | solution.py:52
  234.1 37.4 %fusion.clone.9 = bf16[2560,10240]{0,1:T(8,128)(2,1)} fusion(bf16[384,2560]{1,0:T(8,128)(2,1)} %get-tuple-element.184, bf16[384,20480]{1,0:T(8,128)(2,1)} %get-tuple-element.183, s32[]{:T(128)S(6)} %select_n.27), kind=kOutput, calls=%fused_computation.2.clone.clone.clone.clone.clone.2.clone.1 | convolution fusion | flops 20237516800 | bytes 62259204 | tf_op jit(solution)/shard_map/while/body/eval_jaxpr/dot_general | solution.py:44
  271.6 25.1 %fusion.47 = f32[2560,300]{0,1:T(8,128)} fusion(s32[10240]{0:T(1024)S(1)} %dynamic_slice.28, f32[2560,300]{0,1:T(8,128)} %get-tuple-element.173, pred[]{:T(512)S(6)} %compare.3, bf16[2560,10240]{0,1:T(8,128)(2,1)} %fusion.clone.9), kind=kOutput, calls=%fused_computation.7.clone.3 | convolution fusion | flops 15733248000 | bytes 58613760 | tf_op jit(solution)/shard_map/while/body/eval_jaxpr/dot_general | solution.py:52
  296.7 0.7 copy-done.5
  297.4 40.7 %reduce-scatter.2.cloned.1.call-done = f32[1280,300]{0,1:T(8,128)} async-done(((f32[2560,300]{0,1:T(8,128)}), f32[1280,300]{0,1:T(8,128)}) %reduce-scatter.2.cloned.1.call-update) | async-done | bytes 1536016 | tf_op jit(solution)/shard_map/reduce_scatter | solution.py:84
  338.1 1.6 fusion.26
  339.8 0.6 stack.27
  340.4 0.6 stack.28
  340.9 0.6 stack_broadcast_in_dim.3
  341.5 1.4 stack.29
  342.9 2.1 fusion.12
  345.0 7.0 %psum.14 = f32[300,7]{0,1:T(8,128)S(1)} all-reduce(f32[300,7]{0,1:T(8,128)S(1)} %fusion.12), channel_id=1, replica_groups=mesh['genes'=16,'cols'=2] {'cols'}, use_global_device_ids=true, to_apply=%region_8.9 | all-reduce | flops 2100 | bytes 16800 | tf_op jit(solution)/shard_map/psum | solution.py:86
  352.0 59.6 %psum.15 = f32[300,7]{0,1:T(8,128)S(1)} all-reduce(f32[300,7]{0,1:T(8,128)S(1)} %psum.14), channel_id=1, replica_groups=mesh['genes'=16,'cols'=2] {'genes'}, use_global_device_ids=true, to_apply=%region_9.10 | all-reduce | flops 2100 | bytes 16800 | tf_op jit(solution)/shard_map/psum | solution.py:87
  (33 shorter events, 1.6 us)
Async XLA Ops:
  7.2 1.6 copy-start
  7.2 42.6 %all-gather.6.cloned.1.call-start = ((), (), s32[]{:S(2)}) async-start(), calls=%async_computation.2 | async-start | bytes 2949120 | tf_op jit(solution)/shard_map/all_gather | solution.py:73
  11.5 2.1 copy-start.2
  14.0 2.1 copy-start.3
  15.3 157.2 %all-gather.4.cloned.1.call-start = ((), (), s32[]{:S(2)}) async-start(), calls=%async_computation.1 | async-start | bytes 16711680 | tf_op jit(solution)/shard_map/all_gather | solution.py:79
  16.0 322.1 %reduce-scatter.2.cloned.1.call-start = ((), (), s32[]{:S(2)}) async-start(), calls=%async_computation.3 | async-start | bytes 4669440 | tf_op jit(solution)/shard_map/reduce_scatter | solution.py:84
  296.7 0.7 copy-start.5
  296.7 41.4 %copy-start.4 = (s32[1280,300]{0,1:T(8,128)S(1)}, s32[1280,300]{0,1:T(8,128)}, u32[]{:S(2)}) copy-start(s32[1280,300]{0,1:T(8,128)} %param.8) | copy-start | bytes 4608004
  297.4 114.8 %copy-start.1 = (f32[384,1280]{1,0:T(8,128)S(1)}, f32[384,1280]{1,0:T(8,128)}, u32[]{:S(2)}) copy-start(f32[384,1280]{1,0:T(8,128)} %param.6) | copy-start | bytes 5898244
Sparse Core Ops, SparseCore 0:
  15.4 34.3 all-gather.5
  52.6 119.7 all-gather.3
  296.8 41.1 reduce-scatter.1
